TPU v7x, 8 devices: a whole 2x2x1 slice. The times are simulated.
8 devices in a mesh: data: 2 (over z, y), stage: 4 (over x, core).
Axes of the slice: x: 2, y: 2, z: 1, core: 2. Of those that a mesh axis runs over, the one named last changes fastest.
Arguments:
- x_in: bfloat16 [4, 4, 256, 2048], P(None, 'data')
- g_out: bfloat16 [4, 4, 256, 2048], P(None, 'data')
- w_gate: bfloat16 [4, 1, 2048, 8192], P('stage', None, 'data')
- w_in: bfloat16 [4, 1, 2048, 8192], P('stage', None, 'data')
- w_out: bfloat16 [4, 1, 8192, 2048], P('stage', None, 'data')
Outputs:
- output 1: bfloat16 [4, 4, 256, 2048], P(None, 'data')
- output 2: float32 [4, 1, 2048, 8192], P('stage', None, 'data')
- output 3: float32 [4, 1, 2048, 8192], P('stage', None, 'data')
- output 4: float32 [4, 1, 8192, 2048], P('stage', None, 'data')
All inputs are finite; a program needn't handle non-finite values.
Results may differ from a plain program's by a relative error of at most 0.0134286.
Values are sent between devices in bfloat16 or wider.
A program may use at most 1 GiB of HBM per device.

v0:
```python
import jax
import jax.numpy as jnp
from jax import lax
from jax.sharding import PartitionSpec as P, NamedSharding

EPS = 1e-6


def contract(left_op, right_op, left_dim, right_dim):
    return lax.dot_general(left_op, right_op, (((left_dim,), (right_dim,)), ((), ())), preferred_element_type=jnp.float32)


def rms_parts(h_rows):
    h_f32 = h_rows.astype(jnp.float32)
    inv_rms = lax.rsqrt(jnp.mean(h_f32 * h_f32, axis=-1, keepdims=True) + EPS)
    return h_f32 * inv_rms, inv_rms


def layer_forward(h_rows, gate_w, in_w, out_w):
    normed_f, inv_rms = rms_parts(h_rows)
    normed = normed_f.astype(jnp.bfloat16)
    gate_pre = jnp.dot(normed, gate_w, preferred_element_type=jnp.float32)
    up_pre = jnp.dot(normed, in_w, preferred_element_type=jnp.float32)
    act = (gate_pre * jax.nn.sigmoid(gate_pre) * up_pre).astype(jnp.bfloat16)
    branch = jnp.dot(act, out_w, preferred_element_type=jnp.float32)
    return h_rows + branch.astype(jnp.bfloat16)


def layer_backward(h_rows, d_out, gate_w, in_w, out_w):
    normed_f, inv_rms = rms_parts(h_rows)
    normed = normed_f.astype(jnp.bfloat16)
    gate_pre = jnp.dot(normed, gate_w, preferred_element_type=jnp.float32)
    up_pre = jnp.dot(normed, in_w, preferred_element_type=jnp.float32)
    gate_sig = jax.nn.sigmoid(gate_pre)
    silu_val = gate_pre * gate_sig
    act = (silu_val * up_pre).astype(jnp.bfloat16)
    d_act = contract(d_out, out_w, 1, 1)
    d_out_w = contract(act, d_out, 0, 0)
    d_gate = (d_act * up_pre * gate_sig * (1.0 + gate_pre * (1.0 - gate_sig))).astype(jnp.bfloat16)
    d_up = (d_act * silu_val).astype(jnp.bfloat16)
    d_gate_w = contract(normed, d_gate, 0, 0)
    d_in_w = contract(normed, d_up, 0, 0)
    d_norm = contract(d_gate, gate_w, 1, 1) + contract(d_up, in_w, 1, 1)
    d_res = inv_rms * (d_norm - normed_f * jnp.mean(d_norm * normed_f, axis=-1, keepdims=True))
    d_h = (d_out.astype(jnp.float32) + d_res).astype(jnp.bfloat16)
    return d_h, d_gate_w, d_in_w, d_out_w


def solution(mesh):
    n_stage = mesh.shape["stage"]
    fwd_pairs = [(idx, idx + 1) for idx in range(n_stage - 1)]
    bwd_pairs = [(idx + 1, idx) for idx in range(n_stage - 1)]

    def stage_body(x_loc, g_loc, gate_loc, in_loc, out_loc):
        gate_full = lax.all_gather(gate_loc[0], "data", axis=1, tiled=True)
        in_full = lax.all_gather(in_loc[0], "data", axis=1, tiled=True)
        out_full = lax.all_gather(out_loc[0], "data", axis=1, tiled=True)
        n_layers, d_model, d_ff = gate_full.shape
        weights = [(gate_full[layer], in_full[layer], out_full[layer]) for layer in range(n_layers)]
        n_micro = x_loc.shape[0]
        rows = x_loc.shape[1] * x_loc.shape[2]
        n_steps = n_micro + n_stage - 1
        stage_idx = lax.axis_index("stage")
        is_first = stage_idx == 0
        is_last = stage_idx == n_stage - 1
        x_rows = x_loc.reshape(n_micro, rows, d_model)
        g_rows = g_loc.reshape(n_micro, rows, d_model)

        def fwd_step(carry, step):
            received, saved = carry
            micro_idx = step - stage_idx
            valid = (micro_idx >= 0) & (micro_idx < n_micro)
            slot = jnp.clip(micro_idx, 0, n_micro - 1)
            h_cur = jnp.where(is_first, lax.dynamic_index_in_dim(x_rows, slot, 0, keepdims=False), received)
            layer_inputs = []
            for gate_w, in_w, out_w in weights:
                layer_inputs.append(h_cur)
                h_cur = layer_forward(h_cur, gate_w, in_w, out_w)
            old_vals = lax.dynamic_index_in_dim(saved, slot, 0, keepdims=False)
            new_vals = jnp.where(valid, jnp.stack(layer_inputs), old_vals)
            saved = lax.dynamic_update_index_in_dim(saved, new_vals, slot, 0)
            sent = lax.ppermute(h_cur, "stage", fwd_pairs)
            return (sent, saved), None

        fwd_init = (jnp.zeros((rows, d_model), jnp.bfloat16), jnp.zeros((n_micro, n_layers, rows, d_model), jnp.bfloat16))
        fwd_final, unused = lax.scan(fwd_step, fwd_init, jnp.arange(n_steps))
        saved = fwd_final[1]

        def bwd_step(carry, step):
            received, dx_buf, grad_sums = carry
            micro_idx = step - (n_stage - 1 - stage_idx)
            valid = (micro_idx >= 0) & (micro_idx < n_micro)
            slot = jnp.clip(micro_idx, 0, n_micro - 1)
            d_cur = jnp.where(is_last, lax.dynamic_index_in_dim(g_rows, slot, 0, keepdims=False), received)
            d_cur = jnp.where(valid, d_cur, jnp.zeros_like(d_cur))
            layer_inputs = lax.dynamic_index_in_dim(saved, slot, 0, keepdims=False)
            new_sums = list(grad_sums)
            for layer in reversed(range(n_layers)):
                gate_w, in_w, out_w = weights[layer]
                d_cur, d_gate_w, d_in_w, d_out_w = layer_backward(layer_inputs[layer], d_cur, gate_w, in_w, out_w)
                gate_sum, in_sum, out_sum = new_sums[layer]
                new_sums[layer] = (gate_sum + d_gate_w, in_sum + d_in_w, out_sum + d_out_w)
            old_dx = lax.dynamic_index_in_dim(dx_buf, slot, 0, keepdims=False)
            dx_buf = lax.dynamic_update_index_in_dim(dx_buf, jnp.where(valid & is_first, d_cur, old_dx), slot, 0)
            sent = lax.ppermute(d_cur, "stage", bwd_pairs)
            return (sent, dx_buf, tuple(new_sums)), None

        zero_sums = tuple((jnp.zeros((d_model, d_ff), jnp.float32), jnp.zeros((d_model, d_ff), jnp.float32), jnp.zeros((d_ff, d_model), jnp.float32)) for layer in range(n_layers))
        bwd_init = (jnp.zeros((rows, d_model), jnp.bfloat16), jnp.zeros((n_micro, rows, d_model), jnp.bfloat16), zero_sums)
        bwd_final, unused = lax.scan(bwd_step, bwd_init, jnp.arange(n_steps))
        dx_buf = bwd_final[1]
        grad_sums = bwd_final[2]
        dx_all = lax.psum(dx_buf, "stage").reshape(x_loc.shape)
        gate_grad = lax.psum_scatter(jnp.stack([layer_sums[0] for layer_sums in grad_sums]), "data", scatter_dimension=1, tiled=True)
        in_grad = lax.psum_scatter(jnp.stack([layer_sums[1] for layer_sums in grad_sums]), "data", scatter_dimension=1, tiled=True)
        out_grad = lax.psum_scatter(jnp.stack([layer_sums[2] for layer_sums in grad_sums]), "data", scatter_dimension=1, tiled=True)
        return dx_all, gate_grad[None], in_grad[None], out_grad[None]

    act_spec = P(None, "data", None, None)
    weight_spec = P("stage", None, "data", None)
    return jax.shard_map(stage_body, mesh=mesh, in_specs=(act_spec, act_spec, weight_spec, weight_spec, weight_spec), out_specs=(act_spec, weight_spec, weight_spec, weight_spec), check_vma=False)
```

profile of v0, /device:TPU:0, one launch (start us, length us, event | category | flops | bytes accessed | tf_op | source)
XLA Modules:
  0.0 6519.5 jit_solution(1023285645504321934)
XLA Ops:
  9.5 388.4 %all-gather.7.cloned.1.call-done = bf16[1,1,2048,8192]{3,2,1,0:T(8,128)(2,1)} async-done(((bf16[1,1,1024,8192]{3,2,1,0:T(8,128)(2,1)}), bf16[1,1,2048,8192]{3,2,1,0:T(8,128)(2,1)}) %all-gather.7.cloned.1.call-update) | async-done | bytes 33554448 | tf_op jit(solution)/shard_map/all_gather | solution.py:55
  397.9 387.1 %all-gather.9.cloned.1.call-done = bf16[1,1,2048,8192]{3,2,1,0:T(8,128)(2,1)} async-done(((bf16[1,1,1024,8192]{3,2,1,0:T(8,128)(2,1)}), bf16[1,1,2048,8192]{3,2,1,0:T(8,128)(2,1)}) %all-gather.9.cloned.1.call-update) | async-done | bytes 33554448 | tf_op jit(solution)/shard_map/all_gather | solution.py:56
  784.9 387.1 %all-gather.11.cloned.1.call-done = bf16[1,1,8192,2048]{3,2,1,0:T(8,128)(2,1)} async-done(((bf16[1,1,4096,2048]{3,2,1,0:T(8,128)(2,1)}), bf16[1,1,8192,2048]{3,2,1,0:T(8,128)(2,1)}) %all-gather.11.cloned.1.call-update) | async-done | bytes 33554448 | tf_op jit(solution)/shard_map/all_gather | solution.py:57
  1178.0 819.1 %while.33 = (s32[]{:T(128)}, bf16[512,2048]{1,0:T(8,128)(2,1)}, bf16[4,1,512,2048]{3,2,1,0:T(8,128)(2,1)}, pred[]{:T(512)}, s32[7]{0:T(128)S(1)}, /*index=5*/s32...) while((s32[]{:T(128)}, bf16[512,2048]{1,0:T(8,128)(2,1)}, ...), condition=%wide.region_2.3_spmd, body=%wide.region_0.2_spmd.sunk | while | flops 51578404864 | bytes 192949024 | solution.py:86
  1212.9 31.5 multiply_convert_fusion.clone.8
  1284.1 27.0 fusion.92
  1311.1 31.5 multiply_convert_fusion.clone.8
  1403.8 27.0 fusion.92
  1430.8 31.5 multiply_convert_fusion.clone.8
  1524.0 27.0 fusion.92
  1551.1 31.5 multiply_convert_fusion.clone.8
  1644.3 27.0 fusion.92
  1671.3 31.5 multiply_convert_fusion.clone.8
  1764.5 27.0 fusion.92
  1791.5 31.5 multiply_convert_fusion.clone.8
  1884.8 27.0 fusion.92
  1911.8 31.5 multiply_convert_fusion.clone.8
  2003.7 2138.9 %while.34 = (s32[]{:T(128)}, bf16[512,2048]{1,0:T(8,128)(2,1)}, bf16[4,512,2048]{2,1,0:T(8,128)(2,1)}, f32[2048,8192]{1,0:T(8,128)}, f32[2048,8192]{1,0:T(8,128)...) while((s32[]{:T(128)}, bf16[512,2048]{1,0:T(8,128)(2,1)}, ...), condition=%wide.region_6.7_spmd.clone, body=%wide.region_3.6_spmd.clone.sunk | while | flops 137651814400 | bytes 792750336 | solution.py:110
  2010.8 27.6 fusion.111
  2038.4 27.6 fusion.110
  2068.5 34.1 multiply_convert_fusion.10
  2159.8 29.8 select_add_fusion.7
  2189.6 29.8 select_add_fusion.6
  2219.3 36.2 select_add_fusion.8
  2263.1 27.6 fusion.111
  2290.7 27.6 fusion.110
  2320.7 33.9 multiply_convert_fusion.10
  2412.0 52.3 select_add_fusion.7
  2464.3 52.3 select_add_fusion.6
  2516.6 53.3 select_add_fusion.8
  2577.1 27.6 fusion.111
  2604.8 27.6 fusion.110
  2634.8 34.1 multiply_convert_fusion.10
  2726.1 52.3 select_add_fusion.7
  2778.4 52.3 select_add_fusion.6
  2830.7 53.3 select_add_fusion.8
  2891.5 27.6 fusion.111
  2919.1 27.6 fusion.110
  2949.1 33.9 multiply_convert_fusion.10
  3040.4 52.3 select_add_fusion.7
  3092.7 52.3 select_add_fusion.6
  3145.0 53.3 select_add_fusion.8
  3205.5 27.6 fusion.111
  3233.1 27.6 fusion.110
  3263.2 34.1 multiply_convert_fusion.10
  3354.5 52.3 select_add_fusion.7
  3406.8 52.3 select_add_fusion.6
  3459.1 53.3 select_add_fusion.8
  3519.8 27.6 fusion.111
  3547.4 27.6 fusion.110
  3577.5 33.9 multiply_convert_fusion.10
  3668.8 52.3 select_add_fusion.7
  3721.1 52.3 select_add_fusion.6
  3773.4 53.3 select_add_fusion.8
  3833.9 27.6 fusion.111
  3861.5 27.6 fusion.110
  3891.6 34.1 multiply_convert_fusion.10
  3982.9 52.3 select_add_fusion.7
  4035.2 52.3 select_add_fusion.6
  4087.5 53.3 select_add_fusion.8
  4144.6 174.1 %all-reduce.2.cloned.1.call-done = bf16[4,2,256,2048]{3,2,1,0:T(8,128)(2,1)} async-done(((bf16[4,2,256,2048]{3,2,1,0:T(8,128)(2,1)}), bf16[4,2,256,2048]{3,2,1,0:T(8,128)(2,1)}) %all-reduce.2.cloned.1.call-update) | async-done | bytes 8388624 | tf_op jit(solution)/shard_map/psum | solution.py:113
  4318.7 728.5 %reduce-scatter.8.cloned.1.call-done = f32[1,4096,2048]{2,1,0:T(8,128)} async-done(((f32[1,8192,2048]{2,1,0:T(8,128)}), f32[1,4096,2048]{2,1,0:T(8,128)}) %reduce-scatter.8.cloned.1.call-update) | async-done | bytes 33554448 | tf_op jit(solution)/shard_map/reduce_scatter | solution.py:116
  5047.2 728.3 %reduce-scatter.6.cloned.1.call-done = f32[1,1024,8192]{2,1,0:T(8,128)} async-done(((f32[1,2048,8192]{2,1,0:T(8,128)}), f32[1,1024,8192]{2,1,0:T(8,128)}) %reduce-scatter.6.cloned.1.call-update) | async-done | bytes 33554448 | tf_op jit(solution)/shard_map/reduce_scatter | solution.py:115
  5775.5 728.5 %reduce-scatter.4.cloned.1.call-done = f32[1,1024,8192]{2,1,0:T(8,128)} async-done(((f32[1,2048,8192]{2,1,0:T(8,128)}), f32[1,1024,8192]{2,1,0:T(8,128)}) %reduce-scatter.4.cloned.1.call-update) | async-done | bytes 33554448 | tf_op jit(solution)/shard_map/reduce_scatter | solution.py:114
  (186 shorter events, 920.2 us)
Async XLA Ops:
  7.2 390.7 %all-gather.7.cloned.1.call-start = ((), (), s32[]{:S(2)}) async-start(), calls=%async_computation.7 | async-start | bytes 50331648 | tf_op jit(solution)/shard_map/all_gather | solution.py:55
  7.9 777.0 %all-gather.9.cloned.1.call-start = ((), (), s32[]{:S(2)}) async-start(), calls=%async_computation.8 | async-start | bytes 50331648 | tf_op jit(solution)/shard_map/all_gather | solution.py:56
  8.6 1163.3 %all-gather.11.cloned.1.call-start = ((), (), s32[]{:S(2)}) async-start(), calls=%async_computation.9 | async-start | bytes 50331648 | tf_op jit(solution)/shard_map/all_gather | solution.py:57
  9.4 4309.3 %all-reduce.2.cloned.1.call-start = ((), (), s32[]{:S(2)}) async-start(), calls=%async_computation.3 | async-start | bytes 16777216 | tf_op jit(solution)/shard_map/psum | solution.py:113
  1269.0 5.9 collective-permute-start
  1274.9 1.3 copy-start.1
  1367.1 27.5 collective-permute-start
  1394.6 1.3 copy-start.1
  1486.9 28.0 collective-permute-start
  1514.8 1.3 copy-start.1
  1607.1 28.0 collective-permute-start
  1635.1 1.3 copy-start.1
  1727.4 28.0 collective-permute-start
  1755.3 1.3 copy-start.1
  1847.6 28.0 collective-permute-start
  1875.6 1.3 copy-start.1
  1967.8 28.0 collective-permute-start
  1995.8 1.3 copy-start.1
  2127.4 25.9 copy-start
  2158.5 97.1 %collective-permute-start.1 = (bf16[512,2048]{1,0:T(8,128)(2,1)}, bf16[512,2048]{1,0:T(8,128)(2,1)}, u32[]{:S(2)}, u32[]{:S(2)}) collective-permute-start(bf16[512,2048]{1,0:T(8,128)(2,1)} %get-tuple-element.507), channel_id=1, source_target_pairs={{1,0},{2,1},{3,2},{5,4},{6,5},{7,6}} | collective-permute-start | bytes 6291464 | tf_op jit(solution)/shard_map/while/body/eval_jaxpr/ppermute | solution.py:105
  2379.5 25.9 copy-start
  2410.7 159.1 %collective-permute-start.1 = (bf16[512,2048]{1,0:T(8,128)(2,1)}, bf16[512,2048]{1,0:T(8,128)(2,1)}, u32[]{:S(2)}, u32[]{:S(2)}) collective-permute-start(bf16[512,2048]{1,0:T(8,128)(2,1)} %get-tuple-element.507), channel_id=1, source_target_pairs={{1,0},{2,1},{3,2},{5,4},{6,5},{7,6}} | collective-permute-start | bytes 6291464 | tf_op jit(solution)/shard_map/while/body/eval_jaxpr/ppermute | solution.py:105
  2693.8 25.9 copy-start
  2724.8 159.1 %collective-permute-start.1 = (bf16[512,2048]{1,0:T(8,128)(2,1)}, bf16[512,2048]{1,0:T(8,128)(2,1)}, u32[]{:S(2)}, u32[]{:S(2)}) collective-permute-start(bf16[512,2048]{1,0:T(8,128)(2,1)} %get-tuple-element.507), channel_id=1, source_target_pairs={{1,0},{2,1},{3,2},{5,4},{6,5},{7,6}} | collective-permute-start | bytes 6291464 | tf_op jit(solution)/shard_map/while/body/eval_jaxpr/ppermute | solution.py:105
  3007.8 25.9 copy-start
  3039.1 159.1 %collective-permute-start.1 = (bf16[512,2048]{1,0:T(8,128)(2,1)}, bf16[512,2048]{1,0:T(8,128)(2,1)}, u32[]{:S(2)}, u32[]{:S(2)}) collective-permute-start(bf16[512,2048]{1,0:T(8,128)(2,1)} %get-tuple-element.507), channel_id=1, source_target_pairs={{1,0},{2,1},{3,2},{5,4},{6,5},{7,6}} | collective-permute-start | bytes 6291464 | tf_op jit(solution)/shard_map/while/body/eval_jaxpr/ppermute | solution.py:105
  3322.2 25.9 copy-start
  3353.2 159.1 %collective-permute-start.1 = (bf16[512,2048]{1,0:T(8,128)(2,1)}, bf16[512,2048]{1,0:T(8,128)(2,1)}, u32[]{:S(2)}, u32[]{:S(2)}) collective-permute-start(bf16[512,2048]{1,0:T(8,128)(2,1)} %get-tuple-element.507), channel_id=1, source_target_pairs={{1,0},{2,1},{3,2},{5,4},{6,5},{7,6}} | collective-permute-start | bytes 6291464 | tf_op jit(solution)/shard_map/while/body/eval_jaxpr/ppermute | solution.py:105
  3636.2 25.9 copy-start
  3667.5 159.1 %collective-permute-start.1 = (bf16[512,2048]{1,0:T(8,128)(2,1)}, bf16[512,2048]{1,0:T(8,128)(2,1)}, u32[]{:S(2)}, u32[]{:S(2)}) collective-permute-start(bf16[512,2048]{1,0:T(8,128)(2,1)} %get-tuple-element.507), channel_id=1, source_target_pairs={{1,0},{2,1},{3,2},{5,4},{6,5},{7,6}} | collective-permute-start | bytes 6291464 | tf_op jit(solution)/shard_map/while/body/eval_jaxpr/ppermute | solution.py:105
  3950.5 25.9 copy-start
  3981.6 159.1 %collective-permute-start.1 = (bf16[512,2048]{1,0:T(8,128)(2,1)}, bf16[512,2048]{1,0:T(8,128)(2,1)}, u32[]{:S(2)}, u32[]{:S(2)}) collective-permute-start(bf16[512,2048]{1,0:T(8,128)(2,1)} %get-tuple-element.507), channel_id=1, source_target_pairs={{1,0},{2,1},{3,2},{5,4},{6,5},{7,6}} | collective-permute-start | bytes 6291464 | tf_op jit(solution)/shard_map/while/body/eval_jaxpr/ppermute | solution.py:105
  4142.7 904.5 %reduce-scatter.8.cloned.1.call-start = ((), (), s32[]{:S(2)}) async-start(), calls=%async_computation.6 | async-start | bytes 100663296 | tf_op jit(solution)/shard_map/reduce_scatter | solution.py:116
  4143.3 1632.2 %reduce-scatter.6.cloned.1.call-start = ((), (), s32[]{:S(2)}) async-start(), calls=%async_computation.5 | async-start | bytes 100663296 | tf_op jit(solution)/shard_map/reduce_scatter | solution.py:115
  4143.9 2360.1 %reduce-scatter.4.cloned.1.call-start = ((), (), s32[]{:S(2)}) async-start(), calls=%async_computation.4 | async-start | bytes 100663296 | tf_op jit(solution)/shard_map/reduce_scatter | solution.py:114
Sparse Core Ops, SparseCore 0:
  9.5 388.3 all-gather.6
  399.4 385.4 all-gather.8
  786.4 385.4 all-gather.10
  4142.8 175.8 all-reduce.1
  4321.4 725.7 reduce-scatter.7
  5049.9 725.6 reduce-scatter.5
  5778.4 725.6 reduce-scatter.3
where the time goes:
time: 6530 us; the launch traced here: 6520 us
  waiting for transfers between devices  3550 us (54%)
  matrix products  2600 us (40%)
  starting transfers between devices  157 us (2%)
  other arithmetic  102 us (2%)
  local copies, waits for them, and re-layouts  77 us (1%)
    dot_general x42, matrix products, contract(): lax.dot_general(left_op, right_op, (((left_dim,), (right_dim,)), ((), ())...  1640 us
    reduce_scatter x1, waiting for transfers between devices, stage_body(): lax.psum_scatter(jnp.stack([layer_sums[2] for layer_sums in grad_sums]),...  729 us
    reduce_scatter x1, waiting for transfers between devices, stage_body(): lax.psum_scatter(jnp.stack([layer_sums[0] for layer_sums in grad_sums]),...  728 us
    reduce_scatter x1, waiting for transfers between devices, stage_body(): lax.psum_scatter(jnp.stack([layer_sums[1] for layer_sums in grad_sums]),...  728 us
    all_gather x1, waiting for transfers between devices, stage_body(): gate_full = lax.all_gather(gate_loc[0], 'data', axis=1, tiled=True)  388 us
    all_gather x1, waiting for transfers between devices, stage_body(): out_full = lax.all_gather(out_loc[0], 'data', axis=1, tiled=True)  387 us
    all_gather x1, waiting for transfers between devices, stage_body(): in_full = lax.all_gather(in_loc[0], 'data', axis=1, tiled=True)  387 us
    dot_general x7, matrix products, layer_forward(): up_pre = jnp.dot(normed, in_w, preferred_element_type=jnp.float32)  220 us
  transfers between devices with their start and end apart: 21, of which 14 were waited for; matrix products, arithmetic and copies ran while one was open for 16% of the time, Pallas kernels for 0%

commit v1 on v0

v1 whole, which is shorter than its diff:
```python
import jax
import jax.numpy as jnp
from jax import lax
from jax.experimental import pallas as pl
from jax.experimental.pallas import tpu as pltpu
from jax.sharding import Mesh, PartitionSpec as P

EPS = 1e-6
BF16 = jnp.bfloat16
F32 = jnp.float32
VMEM_LIMIT = 60 * 2**20
AXES = ("data", "x", "core")


def dot_nn(left, right):
    return jnp.dot(left, right, preferred_element_type=F32)


def dot_nt(left, right):
    return lax.dot_general(left, right, (((1,), (1,)), ((), ())), preferred_element_type=F32)


def dot_tn(left, right):
    return lax.dot_general(left, right, (((0,), (0,)), ((), ())), preferred_element_type=F32)


def rms_parts(h_rows):
    h_f32 = h_rows.astype(F32)
    inv_rms = lax.rsqrt(jnp.mean(h_f32 * h_f32, axis=-1, keepdims=True) + EPS)
    return h_f32 * inv_rms, inv_rms


def fwd_kernel(scal, h_ref, g_ref, u_ref, o_ref, *refs):
    out_ref, a_ref, b_ref, s_ref, n_scr, acc = refs[-6:]
    tile = pl.program_id(0)
    tiles = pl.num_programs(0)

    @pl.when(scal[0] == 1)
    def _():
        @pl.when(tile == 0)
        def _():
            n_scr[...] = rms_parts(h_ref[...])[0].astype(BF16)
            acc[...] = jnp.zeros_like(acc)

        a = dot_nn(n_scr[...], g_ref[...])
        b = dot_nn(n_scr[...], u_ref[...])
        s = (a * jax.nn.sigmoid(a) * b).astype(BF16)
        a_ref[...] = a
        b_ref[...] = b

        @pl.when((tile >= tiles // 2) == (scal[1] == 1))
        def _():
            s_ref[...] = s

        acc[...] += dot_nn(s, o_ref[...])

        @pl.when(tile == tiles - 1)
        def _():
            out_ref[...] = h_ref[...] + acc[...].astype(BF16)


def fwd_call(scal, h_rows, gate_w, in_w, out_w, saved, tile_w=512):
    rows, d_model = h_rows.shape
    d_ff = gate_w.shape[1]
    tiles = d_ff // tile_w
    half = tiles // 2
    whole = pl.BlockSpec((rows, d_model), lambda j, sc: (0, 0))
    wide = pl.BlockSpec((rows, tile_w), lambda j, sc: (sc[2], j * sc[0]))
    s_spec = pl.BlockSpec((rows, tile_w), lambda j, sc: (sc[3], jnp.clip(j - sc[1] * half, 0, half - 1) * sc[0]))
    up_spec = pl.BlockSpec((d_model, tile_w), lambda j, sc: (0, j * sc[0]))
    down_spec = pl.BlockSpec((tile_w, d_model), lambda j, sc: (j * sc[0], 0))
    extra = [] if saved is None else list(saved)
    aliases = {} if saved is None else {5: 1, 6: 2, 7: 3}
    return pl.pallas_call(
        fwd_kernel,
        grid_spec=pltpu.PrefetchScalarGridSpec(
            num_scalar_prefetch=1,
            grid=(tiles,),
            in_specs=[whole, up_spec, up_spec, down_spec] + [pl.BlockSpec(memory_space=pl.ANY)] * len(extra),
            out_specs=[whole, wide, wide, s_spec],
            scratch_shapes=[pltpu.VMEM((rows, d_model), BF16), pltpu.VMEM((rows, d_model), F32)],
        ),
        out_shape=[
            jax.ShapeDtypeStruct((rows, d_model), BF16),
            jax.ShapeDtypeStruct((5 * rows, d_ff), F32),
            jax.ShapeDtypeStruct((5 * rows, d_ff), F32),
            jax.ShapeDtypeStruct((5 * rows, d_ff // 2), BF16),
        ],
        input_output_aliases=aliases,
        compiler_params=pltpu.CompilerParams(dimension_semantics=("arbitrary",), vmem_limit_bytes=VMEM_LIMIT),
        cost_estimate=pl.CostEstimate(flops=6 * rows * d_model * d_ff, bytes_accessed=6 * d_model * d_ff, transcendentals=0),
        name="block_forward",
    )(scal, h_rows, gate_w, in_w, out_w, *extra)


def bwd_kernel(scal, e_ref, h_ref, a_ref, b_ref, g_ref, u_ref, o_ref, *refs):
    out_ref, da_ref, db_ref, acc = refs[-4:]
    tile = pl.program_id(0)

    @pl.when(scal[0] == 1)
    def _():
        @pl.when(tile == 0)
        def _():
            acc[...] = jnp.zeros_like(acc)

        a = a_ref[...]
        b = b_ref[...]
        t = dot_nt(e_ref[...], o_ref[...])
        sig = jax.nn.sigmoid(a)
        da = (t * b * sig * (1.0 + a * (1.0 - sig))).astype(BF16)
        db = (t * (a * sig)).astype(BF16)
        da_ref[...] = da
        db_ref[...] = db
        acc[...] += dot_nt(da, g_ref[...]) + dot_nt(db, u_ref[...])

        @pl.when(tile == pl.num_programs(0) - 1)
        def _():
            normed, inv_rms = rms_parts(h_ref[...])
            q = acc[...]
            d_res = inv_rms * (q - normed * jnp.mean(q * normed, axis=-1, keepdims=True))
            out_ref[...] = (e_ref[...].astype(F32) + d_res).astype(BF16)


def bwd_call(scal, e_rows, h_rows, a_all, b_all, gate_w, in_w, out_w, grads, tile_w=512):
    rows, d_model = h_rows.shape
    d_ff = gate_w.shape[1]
    tiles = d_ff // tile_w
    whole = pl.BlockSpec((rows, d_model), lambda j, sc: (0, 0))
    ab_spec = pl.BlockSpec((rows, tile_w), lambda j, sc: (sc[2], j * sc[0]))
    grad_spec = pl.BlockSpec((rows, tile_w), lambda j, sc: (sc[3], j * sc[0]))
    up_spec = pl.BlockSpec((d_model, tile_w), lambda j, sc: (0, j * sc[0]))
    down_spec = pl.BlockSpec((tile_w, d_model), lambda j, sc: (j * sc[0], 0))
    extra = [] if grads is None else list(grads)
    aliases = {} if grads is None else {8: 1, 9: 2}
    return pl.pallas_call(
        bwd_kernel,
        grid_spec=pltpu.PrefetchScalarGridSpec(
            num_scalar_prefetch=1,
            grid=(tiles,),
            in_specs=[whole, whole, ab_spec, ab_spec, up_spec, up_spec, down_spec] + [pl.BlockSpec(memory_space=pl.ANY)] * len(extra),
            out_specs=[whole, grad_spec, grad_spec],
            scratch_shapes=[pltpu.VMEM((rows, d_model), F32)],
        ),
        out_shape=[
            jax.ShapeDtypeStruct((rows, d_model), BF16),
            jax.ShapeDtypeStruct((5 * rows, d_ff), BF16),
            jax.ShapeDtypeStruct((5 * rows, d_ff), BF16),
        ],
        input_output_aliases=aliases,
        compiler_params=pltpu.CompilerParams(dimension_semantics=("arbitrary",), vmem_limit_bytes=VMEM_LIMIT),
        cost_estimate=pl.CostEstimate(flops=6 * rows * d_model * d_ff, bytes_accessed=6 * d_model * d_ff, transcendentals=0),
        name="block_backward",
    )(scal, e_rows, h_rows, a_all, b_all, gate_w, in_w, out_w, *extra)


def redo_kernel(scal, n_ref, e_ref, g_ref, u_ref, o_ref, da_ref, db_ref, s_ref):
    tile = pl.program_id(1)
    a = dot_nn(n_ref[...], g_ref[...])
    b = dot_nn(n_ref[...], u_ref[...])
    t = dot_nt(e_ref[...], o_ref[...])
    sig = jax.nn.sigmoid(a)
    silu = a * sig

    @pl.when((tile >= pl.num_programs(1) // 2) == (scal[0] == 1))
    def _():
        s_ref[...] = (silu * b).astype(BF16)

    da_ref[...] = (t * b * sig * (1.0 + a * (1.0 - sig))).astype(BF16)
    db_ref[...] = (t * silu).astype(BF16)


def redo_call(scal, n_rows, e_rows, gate_w, in_w, out_w, row_block=1024, tile_w=512):
    rows, d_model = n_rows.shape
    d_ff = gate_w.shape[1]
    tiles = d_ff // tile_w
    half = tiles // 2
    row_spec = pl.BlockSpec((row_block, d_model), lambda i, j, sc: (i, 0))
    wide = pl.BlockSpec((row_block, tile_w), lambda i, j, sc: (i, j))
    s_spec = pl.BlockSpec((row_block, tile_w), lambda i, j, sc: (i, jnp.clip(j - sc[0] * half, 0, half - 1)))
    up_spec = pl.BlockSpec((d_model, tile_w), lambda i, j, sc: (0, j))
    down_spec = pl.BlockSpec((tile_w, d_model), lambda i, j, sc: (j, 0))
    return pl.pallas_call(
        redo_kernel,
        grid_spec=pltpu.PrefetchScalarGridSpec(
            num_scalar_prefetch=1,
            grid=(rows // row_block, tiles),
            in_specs=[row_spec, row_spec, up_spec, up_spec, down_spec],
            out_specs=[wide, wide, s_spec],
        ),
        out_shape=[
            jax.ShapeDtypeStruct((rows, d_ff), BF16),
            jax.ShapeDtypeStruct((rows, d_ff), BF16),
            jax.ShapeDtypeStruct((rows, d_ff // 2), BF16),
        ],
        compiler_params=pltpu.CompilerParams(dimension_semantics=("arbitrary", "arbitrary"), vmem_limit_bytes=VMEM_LIMIT),
        cost_estimate=pl.CostEstimate(flops=6 * rows * d_model * d_ff, bytes_accessed=6 * d_model * d_ff, transcendentals=0),
        name="block_redo",
    )(scal, n_rows, e_rows, gate_w, in_w, out_w)


def pair_list(keep, move):
    pairs = []
    for data in range(2):
        for x in range(2):
            for core in range(2):
                if keep(data, x, core):
                    to = move(data, x, core)
                    pairs.append((data * 4 + x * 2 + core, to[0] * 4 + to[1] * 2 + to[2]))
    return pairs


EVERY = lambda d, x, c: True
CORE_SWAP = pair_list(EVERY, lambda d, x, c: (d, x, 1 - c))
DATA_SWAP = pair_list(EVERY, lambda d, x, c: (1 - d, x, c))
DIAG_SWAP = pair_list(EVERY, lambda d, x, c: (1 - d, x, 1 - c))
HOP_UP = pair_list(lambda d, x, c: x == 0, lambda d, x, c: (d, 1, c))
HOP_DOWN = pair_list(lambda d, x, c: x == 1, lambda d, x, c: (d, 0, c))


def move(value, pairs):
    return lax.ppermute(value, AXES, pairs)


def solution(mesh):
    mesh3 = Mesh(mesh.devices.reshape(2, 2, 2), AXES)

    def body(x_loc, g_loc, gate_loc, in_loc, out_loc):
        data = lax.axis_index("data")
        x_pos = lax.axis_index("x")
        core = lax.axis_index("core")
        low = x_pos == 0
        n_micro, batch, seq, d_model = x_loc.shape
        d_ff = gate_loc.shape[-1]
        per_core = n_micro * batch * seq // 2
        chunks = 2
        rows = per_core // chunks

        def pieces(shard):
            half = shard.shape[0] // 2
            mine = lax.dynamic_slice_in_dim(shard, core * half, half, 0)
            other = lax.dynamic_slice_in_dim(shard, (1 - core) * half, half, 0)
            got = move(other, CORE_SWAP)
            return [jnp.where(core == block, mine, got) for block in range(2)]

        parts = [pieces(w[0, 0]) for w in (gate_loc, in_loc, out_loc)]
        weights = [[lax.all_gather(parts[w][block], ("data", "core"), axis=0, tiled=True) for w in range(3)] for block in range(2)]

        x_rows = lax.dynamic_index_in_dim(x_loc, core, 1, keepdims=False).reshape(chunks, rows, d_model)
        g_rows = lax.dynamic_index_in_dim(g_loc, core, 1, keepdims=False).reshape(chunks, rows, d_model)

        def scal_of(valid, block, chunk):
            role = jnp.where(core == block, 0, 1)
            ab_row = jnp.where(valid, block * chunks + chunk, 2 * chunks)
            role_row = jnp.where(valid, role * chunks + chunk, 2 * chunks)
            return jnp.stack([valid.astype(jnp.int32), data, ab_row, role_row]).astype(jnp.int32)

        saved = None
        grads = None

        def forward(valid, block, chunk, h_rows):
            nonlocal saved
            out, *saved = fwd_call(scal_of(valid, block, chunk), h_rows, *weights[block], saved)
            return out

        def backward(valid, block, chunk, e_rows, h_rows):
            nonlocal grads
            out, *grads = bwd_call(scal_of(valid, block, chunk), e_rows, h_rows, saved[0], saved[1], *weights[block], grads)
            return out

        high = jnp.logical_not(low)
        mid_low = [forward(low, 0, ch, x_rows[ch]) for ch in range(chunks)]
        got_up = []
        for ch in range(chunks):
            got_up.append(move(forward(low, 1, ch, mid_low[ch]), HOP_UP))
        h_in = [[None] * chunks, [None] * chunks]
        e_out = [[None] * chunks, [None] * chunks]
        for ch in range(chunks):
            mid = forward(high, 0, ch, got_up[ch])
            forward(high, 1, ch, mid)
            h_in[0][ch] = jnp.where(low, x_rows[ch], got_up[ch])
            h_in[1][ch] = jnp.where(low, mid_low[ch], mid)
        got_down = []
        mid_high = []
        for ch in range(chunks):
            e_mid = backward(high, 1, ch, g_rows[ch], h_in[1][ch])
            mid_high.append(e_mid)
            got_down.append(move(backward(high, 0, ch, e_mid, h_in[0][ch]), HOP_DOWN))
        dx = []
        for ch in range(chunks):
            e_mid = backward(low, 1, ch, got_down[ch], h_in[1][ch])
            dx.append(backward(low, 0, ch, e_mid, h_in[0][ch]))
            e_out[1][ch] = jnp.where(low, got_down[ch], g_rows[ch])
            e_out[0][ch] = jnp.where(low, e_mid, mid_high[ch])

        full = []
        for ch in range(chunks):
            here = jnp.where(low, dx[ch], move(dx[ch], HOP_UP))
            there = move(here, CORE_SWAP)
            pair = jnp.where(core == 0, jnp.stack([here, there]), jnp.stack([there, here]))
            full.append(pair.reshape(batch, n_micro // chunks, seq, d_model).swapaxes(0, 1))
        dx_all = jnp.concatenate(full, axis=0)

        def exchange(values):
            same, cross = [], []
            for ch in range(chunks):
                own = jnp.where(core == 0, values[0][ch], values[1][ch])
                sib = jnp.where(core == 0, values[1][ch], values[0][ch])
                same.append(move(own, DATA_SWAP))
                cross.append(move(sib, DIAG_SWAP))
            return jnp.concatenate(same + cross, axis=0)

        def own_side(values):
            own = jnp.concatenate([jnp.where(core == 0, values[0][ch], values[1][ch]) for ch in range(chunks)], axis=0)
            sib = jnp.concatenate([jnp.where(core == 0, values[1][ch], values[0][ch]) for ch in range(chunks)], axis=0)
            return own, move(sib, CORE_SWAP)

        h_far = exchange(h_in)
        e_far = exchange(e_out)
        n_far = rms_parts(h_far)[0].astype(BF16)
        redo_scal = jnp.stack([data]).astype(jnp.int32)
        da_far, db_far, s_far = lax.cond(
            core == 0,
            lambda: tuple(redo_call(redo_scal, n_far, e_far, *weights[0])),
            lambda: tuple(redo_call(redo_scal, n_far, e_far, *weights[1])),
        )

        h_own, h_sib = own_side(h_in)
        e_own, e_sib = own_side(e_out)
        da_all, db_all = grads
        s_all = saved[2]

        def split(stacked):
            return stacked[:per_core], move(stacked[per_core:2 * per_core], CORE_SWAP)

        da_own, da_sib = split(da_all)
        db_own, db_sib = split(db_all)
        s_own, s_sib = split(s_all)
        col = d_model // 2

        def half_cols(normed):
            return lax.dynamic_slice_in_dim(normed, data * col, col, 1)

        n_own = half_cols(rms_parts(h_own)[0].astype(BF16))
        n_sib = half_cols(rms_parts(h_sib)[0].astype(BF16))
        n_far = half_cols(n_far)

        def weight_grad(lefts, rights):
            left = jnp.concatenate(lefts, axis=0)
            right = jnp.concatenate(rights, axis=0)
            return dot_tn(left, right)

        lefts = [n_own, n_sib, n_far]
        gate_grad = weight_grad(lefts, [da_own, da_sib, da_far])
        in_grad = weight_grad(lefts, [db_own, db_sib, db_far])
        out_grad = weight_grad([s_own, s_sib, s_far], [e_own, e_sib, e_far])
        return dx_all, gate_grad[None, None], in_grad[None, None], out_grad[None, None]

    act_spec = P(None, "data", None, None)
    weight_spec = P(("x", "core"), None, "data", None)
    return jax.shard_map(
        body,
        mesh=mesh3,
        in_specs=(act_spec, act_spec, weight_spec, weight_spec, weight_spec),
        out_specs=(act_spec, weight_spec, weight_spec, weight_spec),
        check_vma=False,
    )
```

time: 6530 us -> 2910 us (0.45)
  matrix products: 2600 us -> 241 us
  waiting for transfers between devices: 3550 us -> 1500 us
  Pallas kernels: 0 us -> 879 us
  starting transfers between devices: 157 us -> 22.5 us
    dot_general x77 -> x3, matrix products: 2600 us -> 241 us  [dot_tn(): lax.dot_general(left, right, (((0,), (0,)), ((), ())), preferred_element_...]
    reduce_scatter x3 -> x0, waiting for transfers between devices: 2190 us -> none  [the longest x1 729 us: stage_body(): lax.psum_scatter(jnp.stack([layer_sums[2] for layer_sums in grad_sums]),...]
    pallas_call x0 -> x17, Pallas kernels: none -> 879 us  [the longest x8 315 us: bwd_call(): pl.pallas_call(bwd_kernel, grid_spec=pltpu.PrefetchScalarGridSpec(num_sca...]
    ppermute x14 -> x24, waiting for transfers between devices: 25.4 us -> 516 us  [move(): return lax.ppermute(value, AXES, pairs)]
    all_gather x3 -> x6, waiting for transfers between devices: 1160 us -> 987 us  [body(): lax.all_gather(parts[w][block], ('data', 'core'), axis=0, tiled=True)]
    psum x1 -> x0, waiting for transfers between devices: 174 us -> none  [stage_body(): dx_all = lax.psum(dx_buf, 'stage').reshape(x_loc.shape)]
    ppermute x14 -> x24, starting transfers between devices: 157 us -> 22.2 us  [move(): return lax.ppermute(value, AXES, pairs)]
    slice x0 -> x5, local copies, waits for them, and re-layouts: none -> 68.7 us  [the longest x3 59.1 us: split(): return (stacked[:per_core], move(stacked[per_core:2 * per_core], CORE_SWAP))]
  transfers between devices with their start and end apart: 21 -> 30, of which waited for: 14 -> 16; matrix products, arithmetic and copies ran while one was open for 16% -> 13% of each run, Pallas kernels for 0% -> 28%
where the time goes in v1:
time: 2910 us; the launch traced here: 2900 us
  waiting for transfers between devices  1500 us (52%)
  Pallas kernels  879 us (30%)
  matrix products  241 us (8%)
  other arithmetic  127 us (4%)
  local copies, waits for them, and re-layouts  117 us (4%)
    all_gather x6, waiting for transfers between devices, body(): lax.all_gather(parts[w][block], ('data', 'core'), axis=0, tiled=True)  987 us
    ppermute x24, waiting for transfers between devices, move(): return lax.ppermute(value, AXES, pairs)  516 us
    pallas_call x8, Pallas kernels, bwd_call(): pl.pallas_call(bwd_kernel, grid_spec=pltpu.PrefetchScalarGridSpec(num_sca...  315 us
    pallas_call x8, Pallas kernels, fwd_call(): pl.pallas_call(fwd_kernel, grid_spec=pltpu.PrefetchScalarGridSpec(num_sca...  309 us
    pallas_call x1, Pallas kernels, redo_call(): pl.pallas_call(redo_kernel, grid_spec=pltpu.PrefetchScalarGridSpec(num_sc...  255 us
    dot_general x3, matrix products, dot_tn(): lax.dot_general(left, right, (((0,), (0,)), ((), ())), preferred_element_...  241 us
    slice x3, local copies, waits for them, and re-layouts, split(): return (stacked[:per_core], move(stacked[per_core:2 * per_core], CORE_SWAP))  59.1 us
  transfers between devices with their start and end apart: 30, of which 16 were waited for; matrix products, arithmetic and copies ran while one was open for 13% of the time, Pallas kernels for 28%

profile of v1, /device:TPU:0, one launch (start us, length us, event | category | flops | bytes accessed | tf_op | source)
XLA Modules:
  0.0 2904.8 jit_solution(220796717521079815)
XLA Ops:
  7.2 7.8 dynamic-slice_bitcast_fusion.2
  15.9 12.8 collective-permute-done
  28.6 12.6 bitcast_select_fusion.4
  41.4 7.8 dynamic-slice_bitcast_fusion.1
  49.5 16.6 collective-permute-done.1
  66.1 10.9 bitcast_select_fusion.2
  77.1 8.4 dynamic-slice_bitcast_fusion
  85.9 12.8 collective-permute-done.2
  98.7 13.4 bitcast_select_fusion
  116.5 4.8 constant_dynamic-slice_fusion.1
  121.3 4.7 constant_dynamic-slice_fusion
  126.1 117.0 %all-gather.7.cloned.1.call-done.g_ref = bf16[2048,8192]{1,0:T(8,128)(2,1)} async-done(((bf16[512,8192]{1,0:T(8,128)(2,1)}), bf16[2048,8192]{1,0:T(8,128)(2,1)}) %all-gather.7.cloned.1.call-update) | async-done | bytes 33554448 | tf_op jit(solution)/shard_map/all_gather | solution.py:246
  243.1 201.5 %all-gather.9.cloned.1.call-done.u_ref = bf16[2048,8192]{1,0:T(8,128)(2,1)} async-done(((bf16[512,8192]{1,0:T(8,128)(2,1)}), bf16[2048,8192]{1,0:T(8,128)(2,1)}) %all-gather.9.cloned.1.call-update) | async-done | bytes 33554448 | tf_op jit(solution)/shard_map/all_gather | solution.py:246
  444.6 200.9 %all-gather.11.cloned.1.call-done.o_ref = bf16[8192,2048]{1,0:T(8,128)(2,1)} async-done(((bf16[2048,2048]{1,0:T(8,128)(2,1)}), bf16[8192,2048]{1,0:T(8,128)(2,1)}) %all-gather.11.cloned.1.call-update) | async-done | bytes 33554448 | tf_op jit(solution)/shard_map/all_gather | solution.py:246
  645.5 68.3 %block_forward.8 = (bf16[512,2048]{1,0:T(8,128)(2,1)}, f32[2560,8192]{1,0:T(8,128)}, f32[2560,8192]{1,0:T(8,128)}, bf16[2560,4096]{1,0:T(8,128)(2,1)}) custom-call(s32[4]{0:T(128)} %get-tuple-element.195.scal, bf16[512,2048]{1,0:T(8,128)(2,1)} %bitcast.82, bf16[2048,8192]{1,0:T(8,128)(2,1)} %all-gather.7.cloned.1.call-done.g_ref, ...), custom_call_target="tpu_custom_call" | custom-call | flops 51539607552 | bytes 100663296 | tf_op jit(solution)/shard_map/block_forward/pallas_call | solution.py:74
  713.8 68.0 %block_forward.9 = (bf16[512,2048]{1,0:T(8,128)(2,1)}, f32[2560,8192]{1,0:T(8,128)}, f32[2560,8192]{1,0:T(8,128)}, bf16[2560,4096]{1,0:T(8,128)(2,1)}) custom-call(s32[4]{0:T(128)} %get-tuple-element.196.scal, bf16[512,2048]{1,0:T(8,128)(2,1)} %bitcast.81, ...), custom_call_target="tpu_custom_call", output_to_operand_aliasing={{1}: (5, {}), {2}: (6, {}), {3}: (7, {})} | custom-call | flops 51539607552 | bytes 100663296 | tf_op jit(solution)/shard_map/block_forward/pallas_call | solution.py:74
  781.8 65.1 %all-gather.13.cloned.1.call-done.g_ref = bf16[2048,8192]{1,0:T(8,128)(2,1)} async-done(((bf16[512,8192]{1,0:T(8,128)(2,1)}), bf16[2048,8192]{1,0:T(8,128)(2,1)}) %all-gather.13.cloned.1.call-update) | async-done | bytes 33554448 | tf_op jit(solution)/shard_map/all_gather | solution.py:246
  846.9 201.3 %all-gather.15.cloned.1.call-done.u_ref = bf16[2048,8192]{1,0:T(8,128)(2,1)} async-done(((bf16[512,8192]{1,0:T(8,128)(2,1)}), bf16[2048,8192]{1,0:T(8,128)(2,1)}) %all-gather.15.cloned.1.call-update) | async-done | bytes 33554448 | tf_op jit(solution)/shard_map/all_gather | solution.py:246
  1048.2 200.8 %all-gather.17.cloned.1.call-done.o_ref = bf16[8192,2048]{1,0:T(8,128)(2,1)} async-done(((bf16[2048,2048]{1,0:T(8,128)(2,1)}), bf16[8192,2048]{1,0:T(8,128)(2,1)}) %all-gather.17.cloned.1.call-update) | async-done | bytes 33554448 | tf_op jit(solution)/shard_map/all_gather | solution.py:246
  1249.0 68.0 %block_forward.10 = (bf16[512,2048]{1,0:T(8,128)(2,1)}, f32[2560,8192]{1,0:T(8,128)}, f32[2560,8192]{1,0:T(8,128)}, bf16[2560,4096]{1,0:T(8,128)(2,1)}) custom-call(s32[4]{0:T(128)} %get-tuple-element.162.scal, bf16[512,2048]{1,0:T(8,128)(2,1)} %get-tuple-element.97.h_ref, ...), custom_call_target="tpu_custom_call", output_to_operand_aliasing={{1}: (5, {}), {2}: (6, {}), {3}: (7, {})} | custom-call | flops 51539607552 | bytes 100663296 | tf_op jit(solution)/shard_map/block_forward/pallas_call | solution.py:74
  1318.3 78.8 %block_forward.11 = (bf16[512,2048]{1,0:T(8,128)(2,1)}, f32[2560,8192]{1,0:T(8,128)}, f32[2560,8192]{1,0:T(8,128)}, bf16[2560,4096]{1,0:T(8,128)(2,1)}) custom-call(s32[4]{0:T(128)} %get-tuple-element.197.scal, bf16[512,2048]{1,0:T(8,128)(2,1)} %get-tuple-element.105.h_ref, ...), custom_call_target="tpu_custom_call", output_to_operand_aliasing={{1}: (5, {}), {2}: (6, {}), {3}: (7, {})} | custom-call | flops 51539607552 | bytes 100663296 | tf_op jit(solution)/shard_map/block_forward/pallas_call | solution.py:74
  1401.0 6.4 block_forward.12
  1407.4 6.4 block_forward.13
  1413.8 30.2 %collective-permute-done.4.h_ref = bf16[512,2048]{1,0:T(8,128)(2,1)} collective-permute-done((bf16[512,2048]{1,0:T(8,128)(2,1)}, bf16[512,2048]{1,0:T(8,128)(2,1)}, u32[]{:S(2)}, u32[]{:S(2)}) %collective-permute-start.4) | collective-permute-done | bytes 2097184 | tf_op jit(solution)/shard_map/ppermute | solution.py:221
  1444.0 6.9 block_forward.14
  1450.9 5.2 broadcast_select_fusion.6
  1460.1 6.5 maximum_convert_fusion
  1471.5 6.4 block_forward.15
  1477.8 7.2 block_backward.8
  1485.0 7.5 block_backward.9
  1493.8 3.3 broadcast_select_fusion.4
  1499.4 7.1 block_backward.10
  1506.6 7.3 block_backward.11
  1513.8 3.9 fusion.30
  1517.7 4.2 pad_maximum_fusion.3
  1521.9 11.7 fusion.38
  1533.6 317.4 %collective-permute-done.5.e_ref = bf16[512,2048]{1,0:T(8,128)(2,1)} collective-permute-done((bf16[512,2048]{1,0:T(8,128)(2,1)}, bf16[512,2048]{1,0:T(8,128)(2,1)}, u32[]{:S(2)}, u32[]{:S(2)}) %collective-permute-start.5) | collective-permute-done | bytes 2097184 | tf_op jit(solution)/shard_map/ppermute | solution.py:221
  1852.3 71.7 %block_backward.12 = (bf16[512,2048]{1,0:T(8,128)(2,1)}, bf16[2560,8192]{1,0:T(8,128)(2,1)}, bf16[2560,8192]{1,0:T(8,128)(2,1)}) custom-call(s32[4]{0:T(128)} %get-tuple-element.162.scal, bf16[512,2048]{1,0:T(8,128)(2,1)} %collective-permute-done.5.e_ref, bf16[512,2048]{1,0:T(8,128)(2,1)} %copy-done.2, ...), custom_call_target="tpu_custom_call", output_to_operand_aliasing={{1}: (8, {}), {2}: (9, {})} | custom-call | flops 51539607552 | bytes 100663296 | tf_op jit(solution)/shard_map/block_backward/pallas_call | solution.py:135
  1924.0 71.5 %block_backward.13 = (bf16[512,2048]{1,0:T(8,128)(2,1)}, bf16[2560,8192]{1,0:T(8,128)(2,1)}, bf16[2560,8192]{1,0:T(8,128)(2,1)}) custom-call(s32[4]{0:T(128)} %get-tuple-element.195.scal, bf16[512,2048]{1,0:T(8,128)(2,1)} %get-tuple-element.137.e_ref, bf16[512,2048]{1,0:T(8,128)(2,1)} %copy-done.1, ...), custom_call_target="tpu_custom_call", output_to_operand_aliasing={{1}: (8, {}), {2}: (9, {})} | custom-call | flops 51539607552 | bytes 100663296 | tf_op jit(solution)/shard_map/block_backward/pallas_call | solution.py:135
  1995.5 4.6 broadcast_select_fusion.1
  2000.1 21.6 collective-permute-done.8.e_ref
  2021.7 71.5 %block_backward.14 = (bf16[512,2048]{1,0:T(8,128)(2,1)}, bf16[2560,8192]{1,0:T(8,128)(2,1)}, bf16[2560,8192]{1,0:T(8,128)(2,1)}) custom-call(s32[4]{0:T(128)} %get-tuple-element.197.scal, bf16[512,2048]{1,0:T(8,128)(2,1)} %collective-permute-done.8.e_ref, bf16[512,2048]{1,0:T(8,128)(2,1)} %get-tuple-element.159.h_ref, ...), custom_call_target="tpu_custom_call", output_to_operand_aliasing={{1}: (8, {}), {2}: (9, {})} | custom-call | flops 51539607552 | bytes 100663296 | tf_op jit(solution)/shard_map/block_backward/pallas_call | solution.py:135
  2093.2 71.3 %block_backward.15 = (bf16[512,2048]{1,0:T(8,128)(2,1)}, bf16[2560,8192]{1,0:T(8,128)(2,1)}, bf16[2560,8192]{1,0:T(8,128)(2,1)}) custom-call(s32[4]{0:T(128)} %get-tuple-element.196.scal, bf16[512,2048]{1,0:T(8,128)(2,1)} %get-tuple-element.144.e_ref, bf16[512,2048]{1,0:T(8,128)(2,1)} %get-tuple-element.158.h_ref, ...), custom_call_target="tpu_custom_call", output_to_operand_aliasing={{1}: (8, {}), {2}: (9, {})} | custom-call | flops 51539607552 | bytes 100663296 | tf_op jit(solution)/shard_map/block_backward/pallas_call | solution.py:135
  2164.5 24.1 fusion.37
  2195.3 5.2 fusion.27
  2204.1 23.3 fusion.36
  2229.5 4.8 fusion.28
  2234.3 3.4 copy-done.6
  2238.3 3.3 convert_element_type.16
  2246.1 34.8 %collective-permute-done.6 = bf16[512,2048]{1,0:T(8,128)(2,1)} collective-permute-done((bf16[512,2048]{1,0:T(8,128)(2,1)S(1)}, bf16[512,2048]{1,0:T(8,128)(2,1)}, u32[]{:S(2)}, u32[]{:S(2)}) %collective-permute-start.6) | collective-permute-done | bytes 2097184 | tf_op jit(solution)/shard_map/ppermute | solution.py:221
  2285.2 4.2 pad_maximum_fusion.11
  2292.1 42.0 %collective-permute-done.19 = bf16[512,2048]{1,0:T(8,128)(2,1)} collective-permute-done((bf16[512,2048]{1,0:T(8,128)(2,1)S(1)}, bf16[512,2048]{1,0:T(8,128)(2,1)}, u32[]{:S(2)}, u32[]{:S(2)}) %collective-permute-start.19) | collective-permute-done | bytes 2097184 | tf_op jit(solution)/shard_map/ppermute | solution.py:221
  2335.2 4.1 pad_maximum_fusion.10
  2341.6 4.2 constant_dynamic-update-slice_fusion.7
  2348.3 4.2 constant_dynamic-update-slice_fusion.5
  2352.5 26.6 collective-permute-done.20
  2381.9 255.4 %conditional.1 = ((bf16[2048,8192]{1,0:T(8,128)(2,1)}, bf16[2048,8192]{1,0:T(8,128)(2,1)}, bf16[2048,4096]{1,0:T(8,128)(2,1)})) conditional(s32[]{:T(128)} %convert_element_type.20, (s32[1]{0:T(128)}, bf16[2048,2048]{1,0:T(8,128)(2,1)}, bf16[2048,2048]{1,0:T(8,128)(2,1)}, bf16[2048,8192]{1,0:T(8,128)(2,1)}, bf16[2048,8192]{1,0:T(8,128)(2,1)}, ...), branch_computations={%region_3.4_spmd, %region_4.5_spmd} | conditional | flops 206158430208 | bytes 100663304 | solution.py:321
  2381.9 255.3 %block_redo.3 = (bf16[2048,8192]{1,0:T(8,128)(2,1)}, bf16[2048,8192]{1,0:T(8,128)(2,1)}, bf16[2048,4096]{1,0:T(8,128)(2,1)}) custom-call(s32[1]{0:T(128)} %get-tuple-element.30.scal, bf16[2048,2048]{1,0:T(8,128)(2,1)} %get-tuple-element.31.n_ref, bf16[2048,2048]{1,0:T(8,128)(2,1)} %get-tuple-element.32.e_ref, bf16[2048,8192]{1,0:T(8,128)(2,1)} %get-tuple-element.33.g_ref, ...), custom_call_target="tpu_custom_call" | custom-call | flops 206158430208 | bytes 100663296 | tf_op jit(solution)/shard_map/cond/branch_1_fun/block_redo/pallas_call | solution.py:182
  2637.4 6.0 fusion.32
  2643.4 6.0 fusion.31
  2649.4 7.6 pad_maximum_fusion
  2657.0 80.9 %fusion.18 = f32[1,1,4096,2048]{3,2,1,0:T(8,128)} fusion(bf16[4096,2048]{1,0:T(8,128)(2,1)} %get-tuple-element.184, bf16[2048,4096]{1,0:T(8,128)(2,1)} %get-tuple-element.153, bf16[1024,4096]{1,0:T(8,128)(2,1)} %collective-permute-done.22, bf16[1024,4096]{1,0:T(8,128)(2,1)} %get-tuple-element.174), kind=kOutput, calls=%fused_computation.20 | convolution fusion | flops 68820140032 | bytes 83886080 | tf_op jit(solution)/shard_map/dot_general | solution.py:24
  2737.9 79.9 %fusion.24 = f32[1,1,1024,8192]{3,2,1,0:T(8,128)} fusion(bf16[2048,8192]{1,0:T(8,128)(2,1)} %get-tuple-element.149, bf16[1024,8192]{1,0:T(8,128)(2,1)} %collective-permute-done.16, bf16[1024,8192]{1,0:T(8,128)(2,1)} %get-tuple-element.166, bf16[4096,1024]{1,0:T(8,128)(2,1)} %pad_maximum_fusion.11), kind=kOutput, calls=%fused_computation.22 | convolution fusion | flops 68920803328 | bytes 109051904 | tf_op jit(solution)/shard_map/dot_general | solution.py:24
  2817.8 79.9 %fusion.21 = f32[1,1,1024,8192]{3,2,1,0:T(8,128)} fusion(bf16[2048,8192]{1,0:T(8,128)(2,1)} %get-tuple-element.151, bf16[1024,8192]{1,0:T(8,128)(2,1)} %collective-permute-done.21, bf16[1024,8192]{1,0:T(8,128)(2,1)} %get-tuple-element.164, bf16[4096,1024]{1,0:T(8,128)(2,1)} %pad_maximum_fusion.10), kind=kOutput, calls=%fused_computation.21 | convolution fusion | flops 68920803328 | bytes 109051904 | tf_op jit(solution)/shard_map/dot_general | solution.py:24
  (118 shorter events, 58.2 us)
Async XLA Ops:
  7.2 235.9 %all-gather.7.cloned.1.call-start = ((), (), s32[]{:S(2)}) async-start(), calls=%async_computation | async-start | bytes 41943040 | tf_op jit(solution)/shard_map/all_gather | solution.py:246
  15.0 13.6 collective-permute-start
  41.3 403.3 %all-gather.9.cloned.1.call-start = ((), (), s32[]{:S(2)}) async-start(), calls=%async_computation.1 | async-start | bytes 41943040 | tf_op jit(solution)/shard_map/all_gather | solution.py:246
  49.1 17.0 collective-permute-start.1
  77.1 568.5 %all-gather.11.cloned.1.call-start = ((), (), s32[]{:S(2)}) async-start(), calls=%async_computation.2 | async-start | bytes 41943040 | tf_op jit(solution)/shard_map/all_gather | solution.py:246
  85.5 13.2 collective-permute-start.2
  112.2 734.7 %all-gather.13.cloned.1.call-start = ((), (), s32[]{:S(2)}) async-start(), calls=%async_computation.3 | async-start | bytes 41943040 | tf_op jit(solution)/shard_map/all_gather | solution.py:246
  112.7 935.4 %all-gather.15.cloned.1.call-start = ((), (), s32[]{:S(2)}) async-start(), calls=%async_computation.4 | async-start | bytes 41943040 | tf_op jit(solution)/shard_map/all_gather | solution.py:246
  113.3 1135.6 %all-gather.17.cloned.1.call-start = ((), (), s32[]{:S(2)}) async-start(), calls=%async_computation.5 | async-start | bytes 41943040 | tf_op jit(solution)/shard_map/all_gather | solution.py:246
  1316.9 82.8 %collective-permute-start.3 = (bf16[512,2048]{1,0:T(8,128)(2,1)}, bf16[512,2048]{1,0:T(8,128)(2,1)S(1)}, u32[]{:S(2)}, u32[]{:S(2)}) collective-permute-start(bf16[512,2048]{1,0:T(8,128)(2,1)} %get-tuple-element.104), channel_id=1, source_target_pairs={{0,2},{1,3},{4,6},{5,7}} | collective-permute-start | bytes 6291464 | tf_op jit(solution)/shard_map/ppermute | solution.py:221
  1397.1 46.8 %collective-permute-start.4 = (bf16[512,2048]{1,0:T(8,128)(2,1)}, bf16[512,2048]{1,0:T(8,128)(2,1)}, u32[]{:S(2)}, u32[]{:S(2)}) collective-permute-start(bf16[512,2048]{1,0:T(8,128)(2,1)} %get-tuple-element.113), channel_id=1, source_target_pairs={{0,2},{1,3},{4,6},{5,7}} | collective-permute-start | bytes 6291464 | tf_op jit(solution)/shard_map/ppermute | solution.py:221
  1399.7 1.3 copy-start.11
  1444.0 7.0 copy-start.5
  1450.9 5.6 copy-start.10
  1450.9 5.6 copy-start.12
  1450.9 5.6 copy-start.13
  1450.9 5.7 copy-start.17
  1456.1 735.9 %collective-permute-start.13 = (bf16[512,2048]{1,0:T(8,128)(2,1)}, bf16[512,2048]{1,0:T(8,128)(2,1)}, u32[]{:S(2)}, u32[]{:S(2)}) collective-permute-start(bf16[512,2048]{1,0:T(8,128)(2,1)} %get-tuple-element.157), channel_id=1, source_target_pairs={{0,4},{1,5},{2,6},{3,7},{4,0},{5,1},{6,2},{7,3}} | collective-permute-start | bytes 6291464 | tf_op jit(solution)/shard_map/ppermute | solution.py:221
  1458.5 11.4 copy-start.1
  1458.5 11.4 copy-start.2
  1458.5 736.1 %collective-permute-start.12 = (bf16[512,2048]{1,0:T(8,128)(2,1)}, bf16[512,2048]{1,0:T(8,128)(2,1)}, u32[]{:S(2)}, u32[]{:S(2)}) collective-permute-start(bf16[512,2048]{1,0:T(8,128)(2,1)} %get-tuple-element.154), channel_id=1, source_target_pairs={{0,4},{1,5},{2,6},{3,7},{4,0},{5,1},{6,2},{7,3}} | collective-permute-start | bytes 6291464 | tf_op jit(solution)/shard_map/ppermute | solution.py:221
  1485.0 8.8 copy-start
  1485.0 13.8 copy-start.21
  1492.5 358.5 %collective-permute-start.5 = (bf16[512,2048]{1,0:T(8,128)(2,1)}, bf16[512,2048]{1,0:T(8,128)(2,1)}, u32[]{:S(2)}, u32[]{:S(2)}) collective-permute-start(bf16[512,2048]{1,0:T(8,128)(2,1)} %get-tuple-element.129), channel_id=1, source_target_pairs={{2,0},{3,1},{6,4},{7,5}} | collective-permute-start | bytes 6291464 | tf_op jit(solution)/shard_map/ppermute | solution.py:221
  1497.0 691.6 %collective-permute-start.15 = (bf16[512,2048]{1,0:T(8,128)(2,1)}, bf16[512,2048]{1,0:T(8,128)(2,1)}, u32[]{:S(2)}, u32[]{:S(2)}) collective-permute-start(bf16[512,2048]{1,0:T(8,128)(2,1)} %broadcast_select_fusion.4), channel_id=1, source_target_pairs={{0,5},{1,4},{2,7},{3,6},{4,1},{5,0},{6,3},{7,2}} | collective-permute-start | bytes 6291464 | tf_op jit(solution)/shard_map/ppermute | solution.py:221
  1497.0 692.1 %collective-permute-start.14 = (bf16[512,2048]{1,0:T(8,128)(2,1)}, bf16[512,2048]{1,0:T(8,128)(2,1)}, u32[]{:S(2)}, u32[]{:S(2)}) collective-permute-start(bf16[512,2048]{1,0:T(8,128)(2,1)} %broadcast_select_fusion.5), channel_id=1, source_target_pairs={{0,5},{1,4},{2,7},{3,6},{4,1},{5,0},{6,3},{7,2}} | collective-permute-start | bytes 6291464 | tf_op jit(solution)/shard_map/ppermute | solution.py:221
  1506.5 7.3 copy-start.22
  1506.5 11.2 copy-start.16
  1851.0 170.7 %collective-permute-start.8 = (bf16[512,2048]{1,0:T(8,128)(2,1)}, bf16[512,2048]{1,0:T(8,128)(2,1)}, u32[]{:S(2)}, u32[]{:S(2)}) collective-permute-start(bf16[512,2048]{1,0:T(8,128)(2,1)} %get-tuple-element.141), channel_id=1, source_target_pairs={{2,0},{3,1},{6,4},{7,5}} | collective-permute-start | bytes 6291464 | tf_op jit(solution)/shard_map/ppermute | solution.py:221
  1924.0 71.5 %copy-start.4 = (bf16[2,1,256,2048]{3,2,1,0:T(8,128)(2,1)S(1)}, bf16[2,1,256,2048]{3,2,1,0:T(8,128)(2,1)}, u32[]{:S(2)}) copy-start(bf16[2,1,256,2048]{3,2,1,0:T(8,128)(2,1)} %get-tuple-element.180) | copy-start | bytes 6291460
  2021.7 207.8 %collective-permute-start.11 = (bf16[1024,2048]{1,0:T(8,128)(2,1)}, bf16[1024,2048]{1,0:T(8,128)(2,1)}, u32[]{:S(2)}, u32[]{:S(2)}) collective-permute-start(bf16[1024,2048]{1,0:T(8,128)(2,1)} %pad_maximum_fusion.3), channel_id=1, source_target_pairs={{0,1},{1,0},{2,3},{3,2},{4,5},{5,4},{6,7},{7,6}} | collective-permute-start | bytes 12582920 | tf_op jit(solution)/shard_map/ppermute | solution.py:221
  2164.5 27.6 copy-start.18
  2164.5 30.2 %copy-start.14 = (bf16[512,2048]{1,0:T(8,128)(2,1)S(1)}, bf16[512,2048]{1,0:T(8,128)(2,1)}, u32[]{:S(2)}) copy-start(bf16[512,2048]{1,0:T(8,128)(2,1)} %get-tuple-element.179) | copy-start | bytes 6291460
  2188.6 11.9 copy-start.3
  2188.6 11.9 copy-start.8
  2188.6 11.9 copy-start.9
  2188.6 468.3 %collective-permute-start.22 = (bf16[1024,4096]{1,0:T(8,128)(2,1)}, bf16[1024,4096]{1,0:T(8,128)(2,1)}, u32[]{:S(2)}, u32[]{:S(2)}) collective-permute-start(bf16[1024,4096]{1,0:T(8,128)(2,1)} %get-tuple-element.175), channel_id=1, source_target_pairs={{0,1},{1,0},{2,3},{3,2},{4,5},{5,4},{6,7},{7,6}} | collective-permute-start | bytes 25165832 | tf_op jit(solution)/shard_map/ppermute | solution.py:221
  2189.2 52.5 %collective-permute-start.9 = (bf16[512,2048]{1,0:T(8,128)(2,1)}, bf16[512,2048]{1,0:T(8,128)(2,1)}, u32[]{:S(2)}, u32[]{:S(2)}) collective-permute-start(bf16[512,2048]{1,0:T(8,128)(2,1)} %get-tuple-element.147), channel_id=1, source_target_pairs={{0,2},{1,3},{4,6},{5,7}} | collective-permute-start | bytes 6291464 | tf_op jit(solution)/shard_map/ppermute | solution.py:221
  2192.0 89.0 %collective-permute-start.6 = (bf16[512,2048]{1,0:T(8,128)(2,1)S(1)}, bf16[512,2048]{1,0:T(8,128)(2,1)}, u32[]{:S(2)}, u32[]{:S(2)}) collective-permute-start(bf16[512,2048]{1,0:T(8,128)(2,1)S(1)} %copy-done.18), channel_id=1, source_target_pairs={{0,2},{1,3},{4,6},{5,7}} | collective-permute-start | bytes 6291464 | tf_op jit(solution)/shard_map/ppermute | solution.py:221
  2194.6 89.4 %collective-permute-start.17 = (bf16[512,2048]{1,0:T(8,128)(2,1)S(1)}, bf16[512,2048]{1,0:T(8,128)(2,1)}, u32[]{:S(2)}, u32[]{:S(2)}) collective-permute-start(bf16[512,2048]{1,0:T(8,128)(2,1)S(1)} %copy-done.14), channel_id=1, source_target_pairs={{0,4},{1,5},{2,6},{3,7},{4,0},{5,1},{6,2},{7,3}} | collective-permute-start | bytes 6291464 | tf_op jit(solution)/shard_map/ppermute | solution.py:221
  2204.1 24.8 copy-start.15
  2229.4 105.8 %collective-permute-start.23 = (bf16[1024,2048]{1,0:T(8,128)(2,1)S(1)}, bf16[1024,2048]{1,0:T(8,128)(2,1)S(1)}, u32[]{:S(2)}, u32[]{:S(2)}) collective-permute-start(bf16[1024,2048]{1,0:T(8,128)(2,1)S(1)} %pad_maximum_fusion.4), channel_id=1, source_target_pairs={{0,1},{1,0},{2,3},{3,2},{4,5},{5,4},{6,7},{7,6}} | collective-permute-start | bytes 12582920 | tf_op jit(solution)/shard_map/ppermute | solution.py:221
  2234.3 3.4 copy-start.6
  2241.6 43.6 %copy-start.7 = (bf16[1024,1024]{1,0:T(8,128)(2,1)S(1)}, bf16[1024,1024]{1,0:T(8,128)(2,1)}, u32[]{:S(2)}) copy-start(bf16[1024,1024]{1,0:T(8,128)(2,1)} %fusion.30) | copy-start | bytes 6291460
  2241.6 48.5 %collective-permute-start.18 = (bf16[512,2048]{1,0:T(8,128)(2,1)S(1)}, bf16[512,2048]{1,0:T(8,128)(2,1)S(1)}, u32[]{:S(2)}, u32[]{:S(2)}) collective-permute-start(bf16[512,2048]{1,0:T(8,128)(2,1)S(1)} %get-tuple-element.177), channel_id=1, source_target_pairs={{0,4},{1,5},{2,6},{3,7},{4,0},{5,1},{6,2},{7,3}} | collective-permute-start | bytes 6291464 | tf_op jit(solution)/shard_map/ppermute | solution.py:221
  2281.0 53.1 %collective-permute-start.19 = (bf16[512,2048]{1,0:T(8,128)(2,1)S(1)}, bf16[512,2048]{1,0:T(8,128)(2,1)}, u32[]{:S(2)}, u32[]{:S(2)}) collective-permute-start(bf16[512,2048]{1,0:T(8,128)(2,1)S(1)} %copy-done.15), channel_id=1, source_target_pairs={{0,5},{1,4},{2,7},{3,6},{4,1},{5,0},{6,3},{7,2}} | collective-permute-start | bytes 6291464 | tf_op jit(solution)/shard_map/ppermute | solution.py:221
  2284.1 453.8 %collective-permute-start.16 = (bf16[1024,8192]{1,0:T(8,128)(2,1)}, bf16[1024,8192]{1,0:T(8,128)(2,1)}, u32[]{:S(2)}, u32[]{:S(2)}) collective-permute-start(bf16[1024,8192]{1,0:T(8,128)(2,1)} %get-tuple-element.167), channel_id=1, source_target_pairs={{0,1},{1,0},{2,3},{3,2},{4,5},{5,4},{6,7},{7,6}} | collective-permute-start | bytes 50331656 | tf_op jit(solution)/shard_map/ppermute | solution.py:221
  2290.2 45.1 %copy-start.19 = (bf16[512,2048]{1,0:T(8,128)(2,1)}, bf16[512,2048]{1,0:T(8,128)(2,1)S(1)}, u32[]{:S(2)}) copy-start(bf16[512,2048]{1,0:T(8,128)(2,1)S(1)} %collective-permute-done.18) | copy-start | bytes 6291460
  2290.2 88.9 %collective-permute-start.20 = (bf16[512,2048]{1,0:T(8,128)(2,1)S(1)}, bf16[512,2048]{1,0:T(8,128)(2,1)S(1)}, u32[]{:S(2)}, u32[]{:S(2)}) collective-permute-start(bf16[512,2048]{1,0:T(8,128)(2,1)S(1)} %get-tuple-element.176), channel_id=1, source_target_pairs={{0,5},{1,4},{2,7},{3,6},{4,1},{5,0},{6,3},{7,2}} | collective-permute-start | bytes 6291464 | tf_op jit(solution)/shard_map/ppermute | solution.py:221
  2334.1 303.2 %collective-permute-start.10 = (bf16[512,2048]{1,0:T(8,128)(2,1)}, bf16[512,2048]{1,0:T(8,128)(2,1)}, u32[]{:S(2)}, u32[]{:S(2)}) collective-permute-start(bf16[512,2048]{1,0:T(8,128)(2,1)} %broadcast_select_fusion.12), channel_id=1, source_target_pairs={{0,1},{1,0},{2,3},{3,2},{4,5},{5,4},{6,7},{7,6}} | collective-permute-start | bytes 6291464 | tf_op jit(solution)/shard_map/ppermute | solution.py:221
  2335.2 308.2 %collective-permute-start.7 = (bf16[512,2048]{1,0:T(8,128)(2,1)}, bf16[512,2048]{1,0:T(8,128)(2,1)}, u32[]{:S(2)}, u32[]{:S(2)}) collective-permute-start(bf16[512,2048]{1,0:T(8,128)(2,1)} %broadcast_select_fusion.13), channel_id=1, source_target_pairs={{0,1},{1,0},{2,3},{3,2},{4,5},{5,4},{6,7},{7,6}} | collective-permute-start | bytes 6291464 | tf_op jit(solution)/shard_map/ppermute | solution.py:221
  2339.3 6.5 copy-start.20
  2379.1 438.7 %collective-permute-start.21 = (bf16[1024,8192]{1,0:T(8,128)(2,1)}, bf16[1024,8192]{1,0:T(8,128)(2,1)}, u32[]{:S(2)}, u32[]{:S(2)}) collective-permute-start(bf16[1024,8192]{1,0:T(8,128)(2,1)} %get-tuple-element.165), channel_id=1, source_target_pairs={{0,1},{1,0},{2,3},{3,2},{4,5},{5,4},{6,7},{7,6}} | collective-permute-start | bytes 50331656 | tf_op jit(solution)/shard_map/ppermute | solution.py:221
Sparse Core Ops, SparseCore 0:
  41.4 201.6 all-gather.6
  245.2 199.3 all-gather.8
  446.1 199.3 all-gather.10
  647.5 199.3 all-gather.12
  848.8 199.3 all-gather.14
  1049.6 199.3 all-gather.16
